TPU v7x, 256 devices: a whole 4x4x8 slice. The times are simulated.
256 devices in a mesh: dp: 32 (over y, z), group: 8 (over x, core).
Axes of the slice: x: 4, y: 4, z: 8, core: 2. Of those that a mesh axis runs over, the one named last changes fastest.
Arguments:
- rewards: bfloat16 [65536, 4096], P(('dp', 'group')), may hold values from -6 to 6
- values: bfloat16 [65536, 4096], P(('dp', 'group')), may hold values from -6 to 6
- lengths: int32 [65536], P(('dp', 'group')), may hold values from 1 to 4096
- decay_rate: float32 [65536], P(('dp', 'group')), may hold values from 3.8146973e-06 to 0.03125
- piece_dest: int32 [32, 32], P('dp'), may hold values from 0 to 31, each once within a row
- row_perm: int32 [512, 128], P(('dp', 'group')), may hold values from 0 to 127, each once within a row
- minibatch: int32 [65536], P(('dp', 'group')), may hold values from 0 to 63
Outputs:
- white_rewards: bfloat16 [65536, 4096], P(('dp', 'group'))
- white_advantage: bfloat16 [65536, 4096], P(('dp', 'group'))
Inputs may be any that keep to these rules, and one draw needn't show every extreme that they name: Each row of piece_dest names every index of dp once. Each row of row_perm names every number below 128 once.
All inputs are finite; a program needn't handle non-finite values.
Results may differ from a plain program's by a relative error of at most 0.0049.
Values may be sent and summed in bfloat16 or wider, within the bound.
No kernel may reach another device: no remote copies, remote signals or barrier semaphores. Data moves between devices by JAX's collectives and lax.ppermute only.
A program may use at most 64 MiB of HBM per device.

v0:
```python
import jax
import jax.numpy as jnp
from jax import lax
from jax.sharding import Mesh
from jax.sharding import PartitionSpec as P

MINIBATCHES = 64
DP_GROUP = ("dp_0", "dp_1", "group_0", "group_1")
DP = ("dp_0", "dp_1")
HIGHEST = lax.Precision.HIGHEST


def over_axes(value, axes):
    for axis in axes:
        value = lax.psum(value, axis)
    return value


def discounted(rewards, values, lengths, decay_rate):
    rows_here, span = rewards.shape
    block = min(128, span)
    blocks_here = span // block
    position = jnp.arange(span, dtype=jnp.int32)
    is_valid = position[None, :] < lengths[:, None]
    next_valid = position[None, :] + 1 < lengths[:, None]
    per_step = jnp.exp(-decay_rate)
    value_f = values.astype(jnp.float32)
    value_next = jnp.concatenate([value_f[:, 1:], jnp.zeros((rows_here, 1), jnp.float32)], axis=1)
    td_error = (
        rewards.astype(jnp.float32)
        + per_step[:, None] * jnp.where(next_valid, value_next, 0.0)
        - value_f
    )
    td_error = jnp.where(is_valid, td_error, 0.0).reshape(rows_here, blocks_here, block)
    offset = jnp.arange(block, dtype=jnp.float32)
    lower_scale = jnp.exp(-decay_rate[:, None] * offset[None, :])
    upper_scale = jnp.exp(decay_rate[:, None] * offset[None, :])
    triangle = (offset[:, None] >= offset[None, :]).astype(jnp.float32)
    scaled = td_error * lower_scale[:, None, :]
    summed = jnp.einsum("rjk,kt->rjt", scaled, triangle, precision=HIGHEST)
    local_part = summed * upper_scale[:, None, :]
    heads = local_part[:, :, 0]
    block_step = jnp.exp(-decay_rate * block)

    def carry_step(carry, head):
        fresh = head + block_step * carry
        return (fresh, fresh)

    final_carry, starts = lax.scan(carry_step, jnp.zeros_like(decay_rate), heads.T, reverse=True)
    next_heads = jnp.concatenate([starts[1:].T, jnp.zeros((rows_here, 1), jnp.float32)], axis=1)
    reach = jnp.exp(-decay_rate[:, None] * (block - offset[None, :]))
    total = local_part + reach[:, None, :] * next_heads[:, :, None]
    return jnp.where(is_valid, total.reshape(rows_here, span), 0.0).astype(jnp.bfloat16)


def by_target(array, piece_dest):
    peers = piece_dest.shape[1]
    target = piece_dest[0]
    slots = jnp.arange(peers, dtype=jnp.int32)
    source_slot = jnp.sum(jnp.where(target[None, :] == slots[:, None], slots[None, :], 0), axis=1)
    pieces = array.reshape((peers, array.shape[0] // peers) + array.shape[1:])
    return jnp.take(pieces, source_slot, axis=0).reshape(array.shape)


def reorder(received, row_perm):
    blocks_here, block = row_perm.shape
    chooser = (row_perm[:, :, None] == jnp.arange(block, dtype=jnp.int32)[None, None, :]).astype(
        jnp.bfloat16
    )

    def permute_one(member):
        shaped = member.reshape(blocks_here, block, member.shape[-1])
        mixed = jnp.einsum("bim,bmc->bic", chooser, shaped, preferred_element_type=jnp.float32)
        return mixed.astype(jnp.bfloat16).reshape(member.shape)

    return tuple((permute_one(member) for member in received))


def whiten(rewards, advantage, lengths, minibatch):
    rows_here, span = rewards.shape
    position = jnp.arange(span, dtype=jnp.int32)
    is_valid = position[None, :] < lengths[:, None]
    counted = lengths.astype(jnp.float32)
    reward_f = jnp.where(is_valid, rewards.astype(jnp.float32), 0.0)
    advantage_f = jnp.where(is_valid, advantage.astype(jnp.float32), 0.0)
    member = (minibatch[:, None] == jnp.arange(MINIBATCHES, dtype=jnp.int32)[None, :]).astype(
        jnp.float32
    )
    row_terms = jnp.stack(
        [
            counted,
            jnp.sum(reward_f, axis=1),
            jnp.sum(advantage_f, axis=1),
            jnp.sum(reward_f * reward_f, axis=1),
            jnp.sum(advantage_f * advantage_f, axis=1),
        ],
        axis=1,
    )
    totals = over_axes(jnp.dot(member.T, row_terms, precision=HIGHEST), DP_GROUP)
    count = jnp.maximum(totals[:, 0], 1.0)
    means = totals[:, 1:3] / count[:, None]
    spreads = totals[:, 3:5] / count[:, None] - means * means
    row_means = jnp.dot(member, means, precision=HIGHEST)
    row_scale = jnp.dot(member, lax.rsqrt(spreads + 1e-05), precision=HIGHEST)
    white_rewards = jnp.where(is_valid, (reward_f - row_means[:, 0:1]) * row_scale[:, 0:1], 0.0)
    white_advantage = jnp.where(
        is_valid, (advantage_f - row_means[:, 1:2]) * row_scale[:, 1:2], 0.0
    )
    return (white_rewards.astype(jnp.bfloat16), white_advantage.astype(jnp.bfloat16))


def local(rewards, values, lengths, decay_rate, piece_dest, row_perm, minibatch):
    blocks_here, block = row_perm.shape
    new_order = (jnp.arange(blocks_here, dtype=jnp.int32)[:, None] * block + row_perm).reshape(-1)
    per_row = jnp.stack([lengths.astype(jnp.float32), decay_rate], axis=1)
    moved_terms = lax.all_to_all(
        by_target(per_row, piece_dest), DP, split_axis=0, concat_axis=0, tiled=True
    )
    moved_terms = jnp.take(moved_terms, new_order, axis=0)
    lengths_here = moved_terms[:, 0].astype(jnp.int32)
    rate_here = moved_terms[:, 1]
    moved_rewards, moved_second = reorder(
        (
            lax.all_to_all(
                by_target(rewards, piece_dest), DP, split_axis=0, concat_axis=0, tiled=True
            ),
            lax.all_to_all(
                by_target(values, piece_dest), DP, split_axis=0, concat_axis=0, tiled=True
            ),
        ),
        row_perm,
    )
    advantage = discounted(moved_rewards, moved_second, lengths_here, rate_here)
    return whiten(moved_rewards, advantage, lengths_here, minibatch)


def solution(mesh):
    finer = Mesh(mesh.devices.reshape(4, 8, 4, 2), ("dp_0", "dp_1", "group_0", "group_1"))
    placed = (
        P(DP_GROUP, None),
        P(DP_GROUP, None),
        P(DP_GROUP),
        P(DP_GROUP),
        P(DP, None),
        P(DP_GROUP, None),
        P(DP_GROUP),
    )
    return jax.shard_map(
        local,
        mesh=finer,
        in_specs=placed,
        out_specs=(P(DP_GROUP, None), P(DP_GROUP, None)),
        check_vma=False,
    )
```

profile of v0, /device:TPU:1, one launch (start us, length us, event | category | flops | bytes accessed | tf_op | source)
XLA Modules:
  0.0 210.3 jit_solution(3992248455712595263)
XLA Ops:
  0.6 0.9 select_reduce_fusion
  2.4 0.8 stack.26
  4.5 12.0 %all-to-all-start = ((f32[32,8,2]{1,2,0:T(2,128)}), f32[32,8,2]{1,2,0:T(2,128)S(1)}, u32[]{:S(2)}, u32[]{:S(2)}) async-start(f32[32,8,2]{1,2,0:T(2,128)} %broadcast_select_fusion.3), calls=%async_computation | async-start | bytes 65536 | tf_op jit(solution)/shard_map/all_to_all | solution.py:116
  16.6 2.0 gather_fusion.2
  18.6 3.6 %gather_fusion.3 = bf16[32,8,4096]{2,1,0:T(8,128)(2,1)} fusion(bf16[32,8,4096]{2,1,0:T(8,128)(2,1)} %bitcast.80, s32[1024]{0:T(1024)S(1)} %pad_clamp_fusion), kind=kCustom, calls=%fused_computation.1.clone | custom fusion | bytes 4194432 | tf_op jit(solution)/shard_map/jit(_take)/gather | solution.py:62
  22.2 4.7 %broadcast_select_fusion = (bf16[32,8,4096]{2,1,0:T(8,128)(2,1)}, bf16[32,8,4096]{2,1,0:T(8,128)(2,1)}) fusion(bf16[32,8,4096]{2,1,0:T(8,128)(2,1)} %gather_fusion.3, pred[32]{0:T(512)(128)(4,1)S(1)} %compare_and_fusion, bf16[32,8,4096]{2,1,0:T(8,128)(2,1)} %gather_fusion.2), kind=kLoop, calls=%fused_computation.37 | loop fusion | flops 2097152 | bytes 8388640 | tf_op jit(solution)/shard_map/jit(_take)/select_n | solution.py:62
  26.8 57.1 %all_to_all.21 = bf16[32,8,4096]{2,1,0:T(8,128)(2,1)} all-to-all(bf16[32,8,4096]{2,1,0:T(8,128)(2,1)} %get-tuple-element.154), channel_id=1, replica_groups=mesh['dp_0'=4,'dp_1'=8,'group_0'=4,'group_1'=2] {'dp_0','dp_1'}, dimensions={0} | all-to-all | bytes 4194304 | tf_op jit(solution)/shard_map/all_to_all | solution.py:127
  83.9 8.2 %all-to-all-start.1 = ((bf16[32,8,4096]{2,1,0:T(8,128)(2,1)}), bf16[32,8,4096]{2,1,0:T(8,128)(2,1)}, u32[]{:S(2)}, u32[]{:S(2)}) async-start(bf16[32,8,4096]{2,1,0:T(8,128)(2,1)} %get-tuple-element.155), calls=%async_computation.1 | async-start | bytes 4194304 | tf_op jit(solution)/shard_map/all_to_all | solution.py:124
  94.0 2.3 %convolution_convert_fusion = bf16[2,128,4096]{2,1,0:T(8,128)(2,1)S(1)} fusion(bf16[2,128,4096]{2,1,0:T(8,128)(2,1)} %bitcast.78, s32[2,128]{1,0:T(2,128)S(1)} %copy-done.6), kind=kOutput, calls=%fused_computation.9 | convolution fusion | flops 269516800 | bytes 4195328 | tf_op jit(solution)/shard_map/bim,bmc->bic/dot_general | solution.py:73
  96.4 1.3 copy-done.1
  98.3 3.1 %slice.58 = f32[256,4095]{1,0:T(8,128)} slice(f32[256,4096]{1,0:T(8,128)S(1)} %bitcast_convert_fusion), slice={[0:256], [1:4096]} | slice | bytes 8386560 | tf_op jit(solution)/shard_map/slice | solution.py:28
  101.5 39.4 %all-to-all-done.1 = bf16[32,8,4096]{2,1,0:T(8,128)(2,1)} async-done(((bf16[32,8,4096]{2,1,0:T(8,128)(2,1)}), bf16[32,8,4096]{2,1,0:T(8,128)(2,1)}, u32[]{:S(2)}, u32[]{:S(2)}) %all-to-all-start.1) | async-done | bytes 2097184 | tf_op jit(solution)/shard_map/all_to_all | solution.py:124
  140.9 3.0 %multiply_reduce_fusion.1 = (f32[2,128]{1,0:T(2,128)S(1)}, f32[2,128]{1,0:T(2,128)S(1)}, f32[2,128,4096]{2,1,0:T(8,128)S(1)}) fusion(s32[2,128]{1,0:T(2,128)S(1)} %bitcast.86, bf16[2,128,4096]{2,1,0:T(8,128)(2,1)} %bitcast.10, s32[2,128]{1,0:T(2,128)S(1)} %copy-done.6), kind=kOutput, calls=%fused_computation.27 | convolution fusion | flops 275807744 | bytes 6295552 | tf_op jit(solution)/shard_map/bim,bmc->bic/dot_general | solution.py:73
  144.3 1.8 fusion.10
  146.2 2.9 %fusion.14 = f32[256,32,128]{0,2,1:T(8,128)S(1)} fusion(f32[256,128]{0,1:T(8,128)S(1)} %get-tuple-element.157, f32[256,128]{1,0:T(8,128)S(1)} %copy.53, f32[256,4096]{1,0:T(8,128)S(1)} %fusion.10), kind=kOutput, calls=%fused_computation.34 | convolution fusion | flops 1612726272 | bytes 8650752 | tf_op jit(solution)/shard_map/rjk,kt->rjt/dot_general | solution.py:40
  149.0 2.0 copy-done.3
  151.1 3.3 %while.17 = (s32[]{:T(128)}, f32[256]{0:T(256)S(1)}, f32[32,256]{1,0:T(8,128)S(1)}, f32[32,256]{1,0:T(8,128)S(1)}, f32[256]{0:T(256)S(1)}, /*index=5*/s32[]{:T(128)}, s32[]{:T(128)}, s32[]{:T(128)}) while((s32[]{:T(128)}, f32[256]{0:T(256)S(1)}, f32[32,256]{1,0:T(8,128)S(1)}, f32[32,256]{1,0:T(8,128)S(1)}, f32[256]{0:T(256)S(1)}, ...), condition=%wide.region_3.5_spmd.clone, body=%wide.region_2.4_spmd.clone.sunk | while | flops 772 | bytes 8307 | solution.py:49
  154.4 5.0 %multiply_reduce_fusion = (f32[256]{0:T(256)S(1)}, f32[256]{0:T(256)S(1)}, bf16[256,32,128]{0,2,1:T(8,128)(2,1)}) fusion(s32[256]{0:T(256)S(1)} %fusion.20, s32[32,128]{1,0:T(8,128)S(1)} %multiply_add_fusion.1, f32[256,32,128]{0,2,1:T(8,128)} %copy-done.3, f32[256,32]{0,1:T(8,128)S(1)} %concatenate.8, f32[256,128]{0,1:T(8,128)S(1)} %get-tuple-element.152), kind=kLoop, calls=%fused_computation.26 | loop fusion | flops 10485248 | bytes 6474752 | tf_op jit(solution)/shard_map/reduce_sum | solution.py:95
  159.6 6.5 %psum.28 = f32[64,5]{0,1:T(8,128)S(1)} all-reduce(f32[64,5]{0,1:T(8,128)S(1)} %fusion.18), channel_id=1, replica_groups=mesh['dp_0'=4,'dp_1'=8,'group_0'=4,'group_1'=2] {'dp_0'}, use_global_device_ids=true, to_apply=%region_7.9 | all-reduce | flops 320 | bytes 2560 | tf_op jit(solution)/shard_map/psum | solution.py:15
  166.1 14.4 %psum.29 = f32[64,5]{0,1:T(8,128)S(1)} all-reduce(f32[64,5]{0,1:T(8,128)S(1)} %psum.28), channel_id=1, replica_groups=mesh['dp_0'=4,'dp_1'=8,'group_0'=4,'group_1'=2] {'dp_1'}, use_global_device_ids=true, to_apply=%region_8.10 | all-reduce | flops 320 | bytes 2560 | tf_op jit(solution)/shard_map/psum | solution.py:15
  180.6 8.5 %psum.30 = f32[64,5]{0,1:T(8,128)S(1)} all-reduce(f32[64,5]{0,1:T(8,128)S(1)} %psum.29), channel_id=1, replica_groups=mesh['dp_0'=4,'dp_1'=8,'group_0'=4,'group_1'=2] {'group_0'}, use_global_device_ids=true, to_apply=%region_9.11 | all-reduce | flops 320 | bytes 2560 | tf_op jit(solution)/shard_map/psum | solution.py:15
  189.0 10.8 %psum.31 = f32[64,5]{0,1:T(8,128)S(1)} all-reduce(f32[64,5]{0,1:T(8,128)S(1)} %psum.30), channel_id=1, replica_groups=mesh['dp_0'=4,'dp_1'=8,'group_0'=4,'group_1'=2] {'group_1'}, use_global_device_ids=true, to_apply=%region_10.12 | all-reduce | flops 320 | bytes 2560 | tf_op jit(solution)/shard_map/psum | solution.py:15
  200.3 4.1 %copy.56 = bf16[256,4096]{1,0:T(8,128)(2,1)} copy(bf16[256,4096]{0,1:T(8,128)(2,1)} %bitcast.79) | data formatting | bytes 4194304 | tf_op jit(solution)/shard_map/reshape | solution.py:53
  204.4 5.9 %select_convert_fusion = (bf16[256,4096]{1,0:T(8,128)(2,1)}, bf16[256,4096]{1,0:T(8,128)(2,1)}) fusion(bf16[256,4096]{1,0:T(8,128)(2,1)} %copy.56, f32[256]{0:T(256)S(1)} %bitcast.89, f32[256]{0:T(256)S(1)} %bitcast.87, s32[256]{0:T(256)S(1)} %fusion.20, f32[256]{0:T(256)S(1)} %bitcast.90, f32[256]{0:T(256)S(1)} %bitcast.88, f32[2,128,4096]{2,1,0:T(8,128)} %copy-done.4), kind=kLoop, calls=%fused_computation.24 | loop fusion | flops 13631488 | bytes 10490880 | tf_op jit(solution)/shard_map/convert_element_type | solution.py:109
  (151 shorter events, 8.1 us)
Async XLA Ops:
  0.6 15.9 %copy-start = (bf16[256,4096]{1,0:T(8,128)(2,1)S(1)}, bf16[256,4096]{1,0:T(8,128)(2,1)}, u32[]{:S(2)}) copy-start(bf16[256,4096]{1,0:T(8,128)(2,1)} %param.11) | copy-start | bytes 6291460
  4.5 22.3 %all-to-all-start = ((f32[32,8,2]{1,2,0:T(2,128)}), f32[32,8,2]{1,2,0:T(2,128)S(1)}, u32[]{:S(2)}, u32[]{:S(2)}) async-start(f32[32,8,2]{1,2,0:T(2,128)} %broadcast_select_fusion.3), calls=%async_computation | async-start | bytes 65536 | tf_op jit(solution)/shard_map/all_to_all | solution.py:116
  26.8 65.3 %copy-start.6 = (s32[2,128]{1,0:T(2,128)S(1)}, s32[2,128]{1,0:T(2,128)}, u32[]{:S(2)}) copy-start(s32[2,128]{1,0:T(2,128)} %param.16) | copy-start | bytes 3076
  83.9 56.9 %all-to-all-start.1 = ((bf16[32,8,4096]{2,1,0:T(8,128)(2,1)}), bf16[32,8,4096]{2,1,0:T(8,128)(2,1)}, u32[]{:S(2)}, u32[]{:S(2)}) async-start(bf16[32,8,4096]{2,1,0:T(8,128)(2,1)} %get-tuple-element.155), calls=%async_computation.1 | async-start | bytes 4194304 | tf_op jit(solution)/shard_map/all_to_all | solution.py:124
  96.4 1.3 copy-start.1
  140.9 3.0 %copy-start.2 = (bf16[2,128,4096]{2,1,0:T(8,128)(2,1)S(1)}, bf16[2,128,4096]{2,1,0:T(8,128)(2,1)}, u32[]{:S(2)}) copy-start(bf16[2,128,4096]{2,1,0:T(8,128)(2,1)} %copy-done.1) | copy-start | bytes 6291460
  140.9 3.5 %copy-start.5 = (f32[256,4095]{1,0:T(8,128)S(1)}, f32[256,4095]{1,0:T(8,128)}, u32[]{:S(2)}) copy-start(f32[256,4095]{1,0:T(8,128)} %slice.58) | copy-start | bytes 12579844
  143.9 2.2 %copy-start.4 = (f32[2,128,4096]{2,1,0:T(8,128)}, f32[2,128,4096]{2,1,0:T(8,128)S(1)}, u32[]{:S(2)}) copy-start(f32[2,128,4096]{2,1,0:T(8,128)S(1)} %get-tuple-element.156) | copy-start | bytes 12582916
  149.0 2.0 copy-start.3
  151.0 8.4 %copy-start.7 = (s32[256]{0:T(256)S(1)}, s32[256]{0:T(256)}, u32[]{:S(2)}) copy-start(s32[256]{0:T(256)} %param.17) | copy-start | bytes 3076
where the time goes:
time: 211 us; the launch traced here: 210 us
  blocking collectives  97.3 us (46%)
  waiting for transfers between devices  39.4 us (19%)
  other arithmetic  21.6 us (10%)
  local copies, waits for them, and re-layouts  21 us (10%)
  starting transfers between devices  20.2 us (10%)
  matrix products  8.91 us (4%)
    all_to_all x1, blocking collectives, local(): lax.all_to_all(by_target(values, piece_dest), DP, split_axis=0, concat_ax...  57.1 us
    psum x4, blocking collectives, over_axes(): value = lax.psum(value, axis)  40.2 us
    all_to_all x1, waiting for transfers between devices, local(): lax.all_to_all(by_target(rewards, piece_dest), DP, split_axis=0, concat_a...  39.4 us
    all_to_all x1, starting transfers between devices, local(): lax.all_to_all(by_target(per_row, piece_dest), DP, split_axis=0, concat_a...  12 us
    all_to_all x1, starting transfers between devices, local(): lax.all_to_all(by_target(rewards, piece_dest), DP, split_axis=0, concat_a...  8.16 us
    gather x3, local copies, waits for them, and re-layouts, by_target(): return jnp.take(pieces, source_slot, axis=0).reshape(array.shape)  6.2 us
    convert_element_type x1, other arithmetic, whiten(): white_advantage.astype(jnp.bfloat16)  5.93 us
    select_n x4, other arithmetic, by_target(): return jnp.take(pieces, source_slot, axis=0).reshape(array.shape)  5.38 us
  transfers between devices with their start and end apart: 2, of which 1 were waited for; matrix products, arithmetic and copies ran while one was open for 9% of the time, Pallas kernels for 0%

commit v1 on v0

--- a/solution.py
+++ b/solution.py
@@ -12,7 +12,7 @@
 
 def over_axes(value, axes):
     for axis in axes:
-        value = lax.psum(value, axis)
+        value = jnp.sum(lax.all_gather(value, axis), axis=0)
     return value
 
 

time: 211 us -> 224 us (1.062)
  blocking collectives: 97.3 us -> 110 us
    all_gather x0 -> x4, blocking collectives: none -> 53 us  [over_axes(): value = jnp.sum(lax.all_gather(value, axis), axis=0)]
    psum x4 -> x0, blocking collectives: 40.2 us -> none  [over_axes(): value = lax.psum(value, axis)]
  transfers between devices with their start and end apart: 2 -> 2, of which waited for: 1 -> 1; matrix products, arithmetic and copies ran while one was open for 9% -> 8% of each run, Pallas kernels for 0% -> 0%
where the time goes in v1:
time: 224 us; the launch traced here: 223 us
  blocking collectives  110 us (49%)
  waiting for transfers between devices  39.4 us (18%)
  other arithmetic  21.6 us (10%)
  local copies, waits for them, and re-layouts  21 us (9%)
  starting transfers between devices  20.2 us (9%)
  matrix products  8.91 us (4%)
    all_to_all x1, blocking collectives, local(): lax.all_to_all(by_target(values, piece_dest), DP, split_axis=0, concat_ax...  57.1 us
    all_gather x4, blocking collectives, over_axes(): value = jnp.sum(lax.all_gather(value, axis), axis=0)  53 us
    all_to_all x1, waiting for transfers between devices, local(): lax.all_to_all(by_target(rewards, piece_dest), DP, split_axis=0, concat_a...  39.4 us
    all_to_all x1, starting transfers between devices, local(): lax.all_to_all(by_target(per_row, piece_dest), DP, split_axis=0, concat_a...  12 us
    all_to_all x1, starting transfers between devices, local(): lax.all_to_all(by_target(rewards, piece_dest), DP, split_axis=0, concat_a...  8.16 us
    gather x3, local copies, waits for them, and re-layouts, by_target(): return jnp.take(pieces, source_slot, axis=0).reshape(array.shape)  6.2 us
    convert_element_type x1, other arithmetic, whiten(): white_advantage.astype(jnp.bfloat16)  5.93 us
    select_n x4, other arithmetic, by_target(): return jnp.take(pieces, source_slot, axis=0).reshape(array.shape)  5.38 us
  transfers between devices with their start and end apart: 2, of which 1 were waited for; matrix products, arithmetic and copies ran while one was open for 8% of the time, Pallas kernels for 0%

profile of v1, /device:TPU:1, one launch (start us, length us, event | category | flops | bytes accessed | tf_op | source)
XLA Modules:
  0.0 223.2 jit_solution(5369558405578611703)
XLA Ops:
  0.6 0.9 select_reduce_fusion
  2.4 0.8 stack.26
  4.5 12.0 %all-to-all-start = ((f32[32,8,2]{1,2,0:T(2,128)}), f32[32,8,2]{1,2,0:T(2,128)S(1)}, u32[]{:S(2)}, u32[]{:S(2)}) async-start(f32[32,8,2]{1,2,0:T(2,128)} %broadcast_select_fusion.3), calls=%async_computation | async-start | bytes 65536 | tf_op jit(solution)/shard_map/all_to_all | solution.py:116
  16.6 2.0 gather_fusion.2
  18.6 3.6 %gather_fusion.3 = bf16[32,8,4096]{2,1,0:T(8,128)(2,1)} fusion(bf16[32,8,4096]{2,1,0:T(8,128)(2,1)} %bitcast.85, s32[1024]{0:T(1024)S(1)} %pad_clamp_fusion), kind=kCustom, calls=%fused_computation.1.clone | custom fusion | bytes 4194432 | tf_op jit(solution)/shard_map/jit(_take)/gather | solution.py:62
  22.2 4.7 %broadcast_select_fusion = (bf16[32,8,4096]{2,1,0:T(8,128)(2,1)}, bf16[32,8,4096]{2,1,0:T(8,128)(2,1)}) fusion(bf16[32,8,4096]{2,1,0:T(8,128)(2,1)} %gather_fusion.3, pred[32]{0:T(512)(128)(4,1)S(1)} %compare_and_fusion, bf16[32,8,4096]{2,1,0:T(8,128)(2,1)} %gather_fusion.2), kind=kLoop, calls=%fused_computation.37 | loop fusion | flops 2097152 | bytes 8388640 | tf_op jit(solution)/shard_map/jit(_take)/select_n | solution.py:62
  26.8 57.1 %all_to_all.21 = bf16[32,8,4096]{2,1,0:T(8,128)(2,1)} all-to-all(bf16[32,8,4096]{2,1,0:T(8,128)(2,1)} %get-tuple-element.154), channel_id=1, replica_groups=mesh['dp_0'=4,'dp_1'=8,'group_0'=4,'group_1'=2] {'dp_0','dp_1'}, dimensions={0} | all-to-all | bytes 4194304 | tf_op jit(solution)/shard_map/all_to_all | solution.py:127
  83.9 8.2 %all-to-all-start.1 = ((bf16[32,8,4096]{2,1,0:T(8,128)(2,1)}), bf16[32,8,4096]{2,1,0:T(8,128)(2,1)}, u32[]{:S(2)}, u32[]{:S(2)}) async-start(bf16[32,8,4096]{2,1,0:T(8,128)(2,1)} %get-tuple-element.155), calls=%async_computation.1 | async-start | bytes 4194304 | tf_op jit(solution)/shard_map/all_to_all | solution.py:124
  94.0 2.3 %convolution_convert_fusion = bf16[2,128,4096]{2,1,0:T(8,128)(2,1)S(1)} fusion(bf16[2,128,4096]{2,1,0:T(8,128)(2,1)} %bitcast.83, s32[2,128]{1,0:T(2,128)S(1)} %copy-done.6), kind=kOutput, calls=%fused_computation.9 | convolution fusion | flops 269516800 | bytes 4195328 | tf_op jit(solution)/shard_map/bim,bmc->bic/dot_general | solution.py:73
  96.4 1.3 copy-done.1
  98.3 3.1 %slice.58 = f32[256,4095]{1,0:T(8,128)} slice(f32[256,4096]{1,0:T(8,128)S(1)} %bitcast_convert_fusion), slice={[0:256], [1:4096]} | slice | bytes 8386560 | tf_op jit(solution)/shard_map/slice | solution.py:28
  101.5 39.4 %all-to-all-done.1 = bf16[32,8,4096]{2,1,0:T(8,128)(2,1)} async-done(((bf16[32,8,4096]{2,1,0:T(8,128)(2,1)}), bf16[32,8,4096]{2,1,0:T(8,128)(2,1)}, u32[]{:S(2)}, u32[]{:S(2)}) %all-to-all-start.1) | async-done | bytes 2097184 | tf_op jit(solution)/shard_map/all_to_all | solution.py:124
  140.9 3.0 %multiply_reduce_fusion.1 = (f32[2,128]{1,0:T(2,128)S(1)}, f32[2,128]{1,0:T(2,128)S(1)}, f32[2,128,4096]{2,1,0:T(8,128)S(1)}) fusion(s32[2,128]{1,0:T(2,128)S(1)} %bitcast.91, bf16[2,128,4096]{2,1,0:T(8,128)(2,1)} %bitcast.10, s32[2,128]{1,0:T(2,128)S(1)} %copy-done.6), kind=kOutput, calls=%fused_computation.27 | convolution fusion | flops 275807744 | bytes 6295552 | tf_op jit(solution)/shard_map/bim,bmc->bic/dot_general | solution.py:73
  144.3 1.8 fusion.10
  146.2 2.9 %fusion.14 = f32[256,32,128]{0,2,1:T(8,128)S(1)} fusion(f32[256,128]{0,1:T(8,128)S(1)} %get-tuple-element.157, f32[256,128]{1,0:T(8,128)S(1)} %copy.53, f32[256,4096]{1,0:T(8,128)S(1)} %fusion.10), kind=kOutput, calls=%fused_computation.34 | convolution fusion | flops 1612726272 | bytes 8650752 | tf_op jit(solution)/shard_map/rjk,kt->rjt/dot_general | solution.py:40
  149.0 2.0 copy-done.3
  151.1 3.3 %while.17 = (s32[]{:T(128)}, f32[256]{0:T(256)S(1)}, f32[32,256]{1,0:T(8,128)S(1)}, f32[32,256]{1,0:T(8,128)S(1)}, f32[256]{0:T(256)S(1)}, /*index=5*/s32[]{:T(128)}, s32[]{:T(128)}, s32[]{:T(128)}) while((s32[]{:T(128)}, f32[256]{0:T(256)S(1)}, f32[32,256]{1,0:T(8,128)S(1)}, f32[32,256]{1,0:T(8,128)S(1)}, f32[256]{0:T(256)S(1)}, ...), condition=%wide.region_3.5_spmd.clone, body=%wide.region_2.4_spmd.clone.sunk | while | flops 772 | bytes 8307 | solution.py:49
  154.4 5.0 %multiply_reduce_fusion = (f32[256]{0:T(256)S(1)}, f32[256]{0:T(256)S(1)}, bf16[256,32,128]{0,2,1:T(8,128)(2,1)}) fusion(s32[256]{0:T(256)S(1)} %fusion.19, s32[32,128]{1,0:T(8,128)S(1)} %multiply_add_fusion.1, f32[256,32,128]{0,2,1:T(8,128)} %copy-done.3, f32[256,32]{0,1:T(8,128)S(1)} %concatenate.8, f32[256,128]{0,1:T(8,128)S(1)} %get-tuple-element.152), kind=kLoop, calls=%fused_computation.26 | loop fusion | flops 10485248 | bytes 6474752 | tf_op jit(solution)/shard_map/reduce_sum | solution.py:95
  159.6 9.1 %all-gather.4 = f32[4,64,5]{1,2,0:T(8,128)S(1)} all-gather(f32[1,64,5]{1,2,0:T(8,128)S(1)} %convolution_bitcast_fusion), channel_id=2, replica_groups=mesh['dp_0'=4,'dp_1'=8,'group_0'=4,'group_1'=2] {'dp_0'}, dimensions={0}, use_global_device_ids=true | all-gather | bytes 6400 | tf_op jit(solution)/shard_map/all_gather | solution.py:15
  168.8 19.2 %all-gather.5 = f32[8,64,5]{1,2,0:T(8,128)S(1)} all-gather(f32[1,64,5]{1,2,0:T(8,128)S(1)} %bitcast.93), channel_id=3, replica_groups=mesh['dp_0'=4,'dp_1'=8,'group_0'=4,'group_1'=2] {'dp_1'}, dimensions={0}, use_global_device_ids=true | all-gather | bytes 11520 | tf_op jit(solution)/shard_map/all_gather | solution.py:15
  188.0 9.5 %all-gather.6 = f32[4,64,5]{1,2,0:T(8,128)S(1)} all-gather(f32[1,64,5]{1,2,0:T(8,128)S(1)} %bitcast.92), channel_id=4, replica_groups=mesh['dp_0'=4,'dp_1'=8,'group_0'=4,'group_1'=2] {'group_0'}, dimensions={0}, use_global_device_ids=true | all-gather | bytes 6400 | tf_op jit(solution)/shard_map/all_gather | solution.py:15
  197.5 15.2 %all-gather.7 = f32[2,64,5]{1,2,0:T(8,128)S(1)} all-gather(f32[1,64,5]{1,2,0:T(8,128)S(1)} %bitcast.94), channel_id=5, replica_groups=mesh['dp_0'=4,'dp_1'=8,'group_0'=4,'group_1'=2] {'group_1'}, dimensions={0}, use_global_device_ids=true | all-gather | bytes 3840 | tf_op jit(solution)/shard_map/all_gather | solution.py:15
  213.2 4.1 %copy.56 = bf16[256,4096]{1,0:T(8,128)(2,1)} copy(bf16[256,4096]{0,1:T(8,128)(2,1)} %bitcast.84) | data formatting | bytes 4194304 | tf_op jit(solution)/shard_map/reshape | solution.py:53
  217.3 5.9 %select_convert_fusion = (bf16[256,4096]{1,0:T(8,128)(2,1)}, bf16[256,4096]{1,0:T(8,128)(2,1)}) fusion(bf16[256,4096]{1,0:T(8,128)(2,1)} %copy.56, f32[256]{0:T(256)S(1)} %bitcast.97, f32[256]{0:T(256)S(1)} %bitcast.95, s32[256]{0:T(256)S(1)} %fusion.19, f32[256]{0:T(256)S(1)} %bitcast.98, f32[256]{0:T(256)S(1)} %bitcast.96, f32[2,128,4096]{2,1,0:T(8,128)} %copy-done.4), kind=kLoop, calls=%fused_computation.24 | loop fusion | flops 13631488 | bytes 10490880 | tf_op jit(solution)/shard_map/convert_element_type | solution.py:109
  (155 shorter events, 8.1 us)
Async XLA Ops:
  0.6 15.9 %copy-start = (bf16[256,4096]{1,0:T(8,128)(2,1)S(1)}, bf16[256,4096]{1,0:T(8,128)(2,1)}, u32[]{:S(2)}) copy-start(bf16[256,4096]{1,0:T(8,128)(2,1)} %param.11) | copy-start | bytes 6291460
  4.5 22.3 %all-to-all-start = ((f32[32,8,2]{1,2,0:T(2,128)}), f32[32,8,2]{1,2,0:T(2,128)S(1)}, u32[]{:S(2)}, u32[]{:S(2)}) async-start(f32[32,8,2]{1,2,0:T(2,128)} %broadcast_select_fusion.3), calls=%async_computation | async-start | bytes 65536 | tf_op jit(solution)/shard_map/all_to_all | solution.py:116
  26.8 65.3 %copy-start.6 = (s32[2,128]{1,0:T(2,128)S(1)}, s32[2,128]{1,0:T(2,128)}, u32[]{:S(2)}) copy-start(s32[2,128]{1,0:T(2,128)} %param.16) | copy-start | bytes 3076
  83.9 56.9 %all-to-all-start.1 = ((bf16[32,8,4096]{2,1,0:T(8,128)(2,1)}), bf16[32,8,4096]{2,1,0:T(8,128)(2,1)}, u32[]{:S(2)}, u32[]{:S(2)}) async-start(bf16[32,8,4096]{2,1,0:T(8,128)(2,1)} %get-tuple-element.155), calls=%async_computation.1 | async-start | bytes 4194304 | tf_op jit(solution)/shard_map/all_to_all | solution.py:124
  96.4 1.3 copy-start.1
  140.9 3.0 %copy-start.2 = (bf16[2,128,4096]{2,1,0:T(8,128)(2,1)S(1)}, bf16[2,128,4096]{2,1,0:T(8,128)(2,1)}, u32[]{:S(2)}) copy-start(bf16[2,128,4096]{2,1,0:T(8,128)(2,1)} %copy-done.1) | copy-start | bytes 6291460
  140.9 3.5 %copy-start.5 = (f32[256,4095]{1,0:T(8,128)S(1)}, f32[256,4095]{1,0:T(8,128)}, u32[]{:S(2)}) copy-start(f32[256,4095]{1,0:T(8,128)} %slice.58) | copy-start | bytes 12579844
  143.9 2.2 %copy-start.4 = (f32[2,128,4096]{2,1,0:T(8,128)}, f32[2,128,4096]{2,1,0:T(8,128)S(1)}, u32[]{:S(2)}) copy-start(f32[2,128,4096]{2,1,0:T(8,128)S(1)} %get-tuple-element.156) | copy-start | bytes 12582916
  149.0 2.0 copy-start.3
  151.0 8.4 %copy-start.7 = (s32[256]{0:T(256)S(1)}, s32[256]{0:T(256)}, u32[]{:S(2)}) copy-start(s32[256]{0:T(256)} %param.17) | copy-start | bytes 3076
